TPU v7x, 128 devices: a whole 4x4x4 slice. The times are simulated.
128 devices in a mesh: row: 8 (over z, core), col: 16 (over y, x).
Axes of the slice: x: 4, y: 4, z: 4, core: 2. Of those that a mesh axis runs over, the one named last changes fastest.
Arguments:
- coefs: float32 [2, 1536, 16384], P(None, 'row', 'col'), may hold values from -600 to 600, as said below
- tilts: int32 [1536, 2], replicated, may hold values from 8 to 48
- start_basis: float32 [1536, 32], P('col'), may hold values from -6 to 6
Outputs:
- ccc: float32 [1536, 1536], P('row', 'col')
- basis: float32 [1536, 32], P('col')
Inputs may be any that keep to these rules, and one draw needn't show every extreme that they name: `coefs`: real and imaginary parts are products of a particle scale, a coefficient scale and a bounded random value.
All inputs are finite; a program needn't handle non-finite values.
Results may differ from a plain program's by a relative error of at most 0.0003.
Values sent between devices are 32-bit elements; how exact they have to be, the bound alone decides.
A program may use at most 192 MiB of HBM per device.

v0:
```python
import math
import jax
import jax.numpy as jnp
from jax import lax
from jax.sharding import PartitionSpec as P

GRID = 32
ITERS = 4
EPS = 1e-06
HIGH = lax.Precision.HIGHEST


def in_blocks(array, dim, devices):
    before, after = (array.shape[:dim], array.shape[dim + 1 :])
    return jnp.moveaxis(array.reshape(*before, devices, -1, *after), dim, 0)


def sum_at_owner(array, axis, dim):
    tiles = in_blocks(array, dim, lax.axis_size(axis))
    arrived = lax.all_to_all(tiles, axis, split_axis=0, concat_axis=0, tiled=True)
    return arrived.sum(axis=0)


def from_everyone(array, axis):
    copies = jnp.broadcast_to(array, (lax.axis_size(axis), *array.shape))
    return lax.all_to_all(copies, axis, split_axis=0, concat_axis=0, tiled=True)


def over_copies(array, axis):
    return from_everyone(array, axis).sum(axis=0)


def laid_out(tiles, dim):
    dims = list(tiles.shape[1:])
    dims[dim] *= tiles.shape[0]
    return jnp.moveaxis(tiles, 0, dim).reshape(dims)


def gather_directly(array, axis, dim):
    return laid_out(from_everyone(array, axis), dim)


def wedge(tilt_rows, wave_index):
    wave_x = jnp.abs(wave_index // (GRID * (GRID // 2)) - GRID // 2)[None, :]
    wave_z = (wave_index % GRID - GRID // 2)[None, :]
    upward = wave_z * 16 <= tilt_rows[:, 1:2] * wave_x
    downward = -wave_z * 16 <= tilt_rows[:, 0:1] * wave_x
    return jnp.where(wave_z >= 0, upward, downward).astype(jnp.float32)


def inner(left, right):
    return lax.dot_general(
        left, right, (((1,), (1,)), ((), ())), precision=HIGH, preferred_element_type=jnp.float32
    )


def prepare(values, tilt_rows, wave_index):
    masks = wedge(tilt_rows, wave_index)
    paired = jnp.concatenate([values[0] * masks, values[1] * masks], axis=1)
    energy = masks * (values[0] * values[0] + values[1] * values[1])
    return (masks, paired, energy)


def local(coefs, tilts, start_basis):
    row_count = coefs.shape[1]
    slice_width = coefs.shape[2]
    col_count = start_basis.shape[0]
    col_size = lax.axis_size("col")
    total = col_count * col_size
    row_index = lax.axis_index("row")
    col_index = lax.axis_index("col")
    own_tilts = lax.dynamic_slice_in_dim(tilts, row_index * row_count, row_count, 0)
    wave_index = col_index * slice_width + jnp.arange(slice_width, dtype=jnp.int32)
    own_mask, own_pair, own_energy = prepare(coefs, own_tilts, wave_index)
    gathered = lax.all_gather(coefs, "row", axis=1, tiled=True)
    mask_j, pair_j, energy_j = prepare(gathered, tilts, wave_index)
    numer = inner(pair_j, own_pair)
    first = inner(mask_j, own_energy)
    second = inner(energy_j, own_mask)
    summed = sum_at_owner(jnp.concatenate([numer, first, second], axis=1), "col", 0)
    numer = summed[:, :row_count]
    first = summed[:, row_count : 2 * row_count]
    second = summed[:, 2 * row_count :]
    block = (numer / jnp.sqrt(first * second + EPS)).T
    current = start_basis
    for step in range(ITERS):
        partial_value = jnp.dot(block, current, precision=HIGH, preferred_element_type=jnp.float32)
        summed_rows = over_copies(partial_value, "col")
        local_gram = lax.dot_general(
            summed_rows,
            summed_rows,
            (((0,), (0,)), ((), ())),
            precision=HIGH,
            preferred_element_type=jnp.float32,
        )
        gram = over_copies(local_gram, "row")
        factor = jnp.linalg.cholesky(gram)
        fresh = lax.linalg.triangular_solve(
            factor, summed_rows, left_side=False, lower=True, transpose_a=True
        )
        whole = gather_directly(fresh, "row", 0)
        current = lax.dynamic_slice_in_dim(whole, col_index * col_count, col_count, 0)
    return (block, current * math.sqrt(total))


def solution(mesh):
    in_specs = (P(None, "row", "col"), P(), P("col", None))
    out_specs = (P("row", "col"), P("col", None))
    return jax.shard_map(local, mesh=mesh, in_specs=in_specs, out_specs=out_specs, check_vma=False)
```

profile of v0, /device:TPU:1, one launch (start us, length us, event | category | flops | bytes accessed | tf_op | source)
XLA Modules:
  0.0 345.3 jit_solution(13841363534144779767)
XLA Ops:
  7.9 0.8 fusion.70
  9.6 2.9 bitcast_select_fusion.1
  12.5 7.3 %fusion.18 = f32[1536,192]{0,1:T(8,128)} fusion(f32[2,192,1024]{2,1,0:T(8,128)} %param.6, s32[192]{0:T(256)S(1)} %bitcast.109, s32[1024]{0:T(1024)S(1)} %get-tuple-element.21, s32[1024]{0:T(1024)S(1)} %get-tuple-element.20, s32[192]{0:T(256)S(1)} %bitcast.106, s32[1024]{0:T(1024)S(1)} %broadcast_multiply_fusion, ...), kind=kOutput, calls=%fused_computation.29 | convolution fusion | flops 3633512448 | bytes 2797568 | tf_op jit(solution)/shard_map/dot_general | solution.py:52
  19.8 61.0 %all-gather.2.cloned.1.call-done = f32[2,1536,1024]{2,1,0:T(8,128)} async-done(((f32[2,192,1024]{2,1,0:T(8,128)}), f32[2,1536,1024]{2,1,0:T(8,128)}) %all-gather.2.cloned.1.call-update) | async-done | bytes 12582928 | tf_op jit(solution)/shard_map/all_gather | solution.py:75
  80.8 7.4 %fusion.10 = (f32[1536,1024]{1,0:T(8,128)S(1)}, f32[1536,1024]{1,0:T(8,128)S(1)}) fusion(f32[2,1536,1024]{2,1,0:T(8,128)} %all-gather.2.cloned.1.call-done, s32[1536]{0:T(1024)S(1)} %get-tuple-element.13, s32[1024]{0:T(1024)S(1)} %get-tuple-element.21, s32[1024]{0:T(1024)S(1)} %get-tuple-element.20, s32[1536]{0:T(1024)S(1)} %get-tuple-element.12, ...), kind=kLoop, calls=%fused_computation.14 | loop fusion | flops 11010048 | bytes 25191424 | tf_op jit(solution)/shard_map/mul | solution.py:59
  88.2 15.6 %fusion = f32[1536,192]{0,1:T(8,128)} fusion(f32[1536,1024]{1,0:T(8,128)S(1)} %get-tuple-element.15, f32[1536,1024]{1,0:T(8,128)S(1)} %get-tuple-element.14, f32[192,1024]{1,0:T(8,128)} %get-tuple-element.17, f32[192,1024]{1,0:T(8,128)} %get-tuple-element.16), kind=kOutput, calls=%fused_computation | convolution fusion | flops 7251296256 | bytes 15335424 | tf_op jit(solution)/shard_map/dot_general | solution.py:52
  103.9 6.2 %fusion.4 = f32[1536,192]{0,1:T(8,128)S(1)} fusion(f32[2,1536,1024]{2,1,0:T(8,128)S(1)} %bitcast.104, s32[192]{0:T(256)S(1)} %bitcast.110, s32[1024]{0:T(1024)S(1)} %get-tuple-element.21, s32[1024]{0:T(1024)S(1)} %get-tuple-element.20, s32[192]{0:T(256)S(1)} %bitcast.107, s32[1024]{0:T(1024)S(1)} %broadcast_multiply_fusion, ...), kind=kOutput, calls=%fused_computation.6 | convolution fusion | flops 3639017472 | bytes 13807616 | tf_op jit(solution)/shard_map/dot_general | solution.py:52
  110.4 3.1 copy.54
  113.5 54.3 %all_to_all.65 = f32[16,96,576]{2,1,0:T(8,128)} all-to-all(f32[16,96,576]{2,1,0:T(8,128)} %bitcast.102), channel_id=1, replica_groups=mesh['row'=8,'col'=16] {'col'}, dimensions={0} | all-to-all | bytes 7077888 | tf_op jit(solution)/shard_map/all_to_all | solution.py:20
  167.8 2.3 reduce_sum.81
  170.5 13.4 %all_to_all.66 = f32[16,192,32]{1,2,0:T(8,128)S(1)} all-to-all(f32[16,192,32]{1,2,0:T(8,128)S(1)} %broadcast_in_dim.59), channel_id=1, replica_groups=mesh['row'=8,'col'=16] {'col'}, dimensions={0} | all-to-all | bytes 786432 | tf_op jit(solution)/shard_map/all_to_all | solution.py:26
  184.3 10.0 %all_to_all.67 = f32[8,1,1024]{2,1,0:T(1,128)S(1)} all-to-all(f32[8,1,1024]{2,1,0:T(1,128)S(1)} %reshape.98), channel_id=1, replica_groups=mesh['row'=8,'col'=16] {'row'}, dimensions={0} | all-to-all | bytes 65536 | tf_op jit(solution)/shard_map/all_to_all | solution.py:26
  195.7 2.9 cholesky.74
  199.9 2.4 custom-call.8
  203.3 4.0 %all-to-all-start.3 = ((f32[8,192,32]{1,2,0:T(8,128)}), f32[8,192,32]{1,2,0:T(8,128)S(1)}, u32[]{:S(2)}, u32[]{:S(2)}) async-start(f32[8,192,32]{1,2,0:T(8,128)} %broadcast_in_dim.61), calls=%async_computation.3 | async-start | bytes 524288 | tf_op jit(solution)/shard_map/all_to_all | solution.py:26
  207.4 6.5 %all-to-all-done.3 = f32[8,192,32]{1,2,0:T(8,128)S(1)} async-done(((f32[8,192,32]{1,2,0:T(8,128)}), f32[8,192,32]{1,2,0:T(8,128)S(1)}, u32[]{:S(2)}, u32[]{:S(2)}) %all-to-all-start.3) | async-done | bytes 196640 | tf_op jit(solution)/shard_map/all_to_all | solution.py:26
  214.4 13.0 %all_to_all.68 = f32[16,192,32]{1,2,0:T(8,128)S(1)} all-to-all(f32[16,192,32]{1,2,0:T(8,128)S(1)} %broadcast_in_dim.62), channel_id=1, replica_groups=mesh['row'=8,'col'=16] {'col'}, dimensions={0} | all-to-all | bytes 786432 | tf_op jit(solution)/shard_map/all_to_all | solution.py:26
  227.8 9.2 %all_to_all.69 = f32[8,1,1024]{2,1,0:T(1,128)S(1)} all-to-all(f32[8,1,1024]{2,1,0:T(1,128)S(1)} %reshape.100), channel_id=1, replica_groups=mesh['row'=8,'col'=16] {'row'}, dimensions={0} | all-to-all | bytes 65536 | tf_op jit(solution)/shard_map/all_to_all | solution.py:26
  238.0 2.9 cholesky.85
  242.2 2.4 custom-call.9
  244.9 9.6 %all_to_all.70 = f32[8,192,32]{1,2,0:T(8,128)S(1)} all-to-all(f32[8,192,32]{1,2,0:T(8,128)S(1)} %broadcast_in_dim.64), channel_id=1, replica_groups=mesh['row'=8,'col'=16] {'row'}, dimensions={0} | all-to-all | bytes 393216 | tf_op jit(solution)/shard_map/all_to_all | solution.py:26
  255.1 13.0 %all_to_all.71 = f32[16,192,32]{1,2,0:T(8,128)S(1)} all-to-all(f32[16,192,32]{1,2,0:T(8,128)S(1)} %broadcast_in_dim.65), channel_id=1, replica_groups=mesh['row'=8,'col'=16] {'col'}, dimensions={0} | all-to-all | bytes 786432 | tf_op jit(solution)/shard_map/all_to_all | solution.py:26
  268.5 9.2 %all_to_all.72 = f32[8,1,1024]{2,1,0:T(1,128)S(1)} all-to-all(f32[8,1,1024]{2,1,0:T(1,128)S(1)} %reshape.102), channel_id=1, replica_groups=mesh['row'=8,'col'=16] {'row'}, dimensions={0} | all-to-all | bytes 65536 | tf_op jit(solution)/shard_map/all_to_all | solution.py:26
  278.6 2.9 cholesky.96
  282.9 2.4 custom-call.10
  285.6 9.6 %all_to_all.73 = f32[8,192,32]{1,2,0:T(8,128)S(1)} all-to-all(f32[8,192,32]{1,2,0:T(8,128)S(1)} %broadcast_in_dim.67), channel_id=1, replica_groups=mesh['row'=8,'col'=16] {'row'}, dimensions={0} | all-to-all | bytes 393216 | tf_op jit(solution)/shard_map/all_to_all | solution.py:26
  295.8 13.0 %all_to_all.74 = f32[16,192,32]{1,2,0:T(8,128)S(1)} all-to-all(f32[16,192,32]{1,2,0:T(8,128)S(1)} %broadcast_in_dim.68), channel_id=1, replica_groups=mesh['row'=8,'col'=16] {'col'}, dimensions={0} | all-to-all | bytes 786432 | tf_op jit(solution)/shard_map/all_to_all | solution.py:26
  309.2 9.2 %all_to_all.75 = f32[8,1,1024]{2,1,0:T(1,128)S(1)} all-to-all(f32[8,1,1024]{2,1,0:T(1,128)S(1)} %reshape.104), channel_id=1, replica_groups=mesh['row'=8,'col'=16] {'row'}, dimensions={0} | all-to-all | bytes 65536 | tf_op jit(solution)/shard_map/all_to_all | solution.py:26
  319.3 2.9 cholesky.107
  323.6 2.4 custom-call.11
  327.0 4.0 %all-to-all-start.12 = ((f32[8,192,32]{1,2,0:T(8,128)}), f32[8,192,32]{1,2,0:T(8,128)S(1)}, u32[]{:S(2)}, u32[]{:S(2)}) async-start(f32[8,192,32]{1,2,0:T(8,128)} %broadcast_in_dim.70), calls=%async_computation.12 | async-start | bytes 524288 | tf_op jit(solution)/shard_map/all_to_all | solution.py:26
  331.9 5.6 %all-to-all-done.12 = f32[8,192,32]{1,2,0:T(8,128)S(1)} async-done(((f32[8,192,32]{1,2,0:T(8,128)}), f32[8,192,32]{1,2,0:T(8,128)S(1)}, u32[]{:S(2)}, u32[]{:S(2)}) %all-to-all-start.12) | async-done | bytes 196640 | tf_op jit(solution)/shard_map/all_to_all | solution.py:26
  (97 shorter events, 18.8 us)
Async XLA Ops:
  7.2 163.1 %copy-start = (f32[96,32]{0,1:T(8,128)S(1)}, f32[96,32]{0,1:T(8,128)}, u32[]{:S(2)}) copy-start(f32[96,32]{0,1:T(8,128)} %param.8) | copy-start | bytes 36868
  7.2 73.6 %all-gather.2.cloned.1.call-start = ((), (), s32[]{:S(2)}) async-start(), calls=%async_computation.13 | async-start | bytes 14155776 | tf_op jit(solution)/shard_map/all_gather | solution.py:75
  80.8 23.1 %slice-start = ((s8[12582912]{0:T(1024)(128)(4,1)}), s8[4194304]{0:T(1024)(128)(4,1)S(1)}, s32[]{:S(2)}) async-start(s8[12582912]{0:T(1024)(128)(4,1)} %bitcast.103), calls=%async_computation.14 | async-start | bytes 8388608
  80.8 23.1 %slice-start.1 = ((s8[12582912]{0:T(1024)(128)(4,1)}), s8[4194304]{0:T(1024)(128)(4,1)S(1)}, s32[]{:S(2)}) async-start(s8[12582912]{0:T(1024)(128)(4,1)} %bitcast.103), calls=%async_computation.15 | async-start | bytes 8388608
  88.2 15.7 %slice-start.2 = ((s8[12582912]{0:T(1024)(128)(4,1)}), s8[4194304]{0:T(1024)(128)(4,1)S(1)}, s32[]{:S(2)}) async-start(s8[12582912]{0:T(1024)(128)(4,1)} %bitcast.103), calls=%async_computation.16 | async-start | bytes 8388608
  103.9 6.2 %copy-start.1 = (f32[1536,192]{0,1:T(8,128)S(1)}, f32[1536,192]{0,1:T(8,128)}, u32[]{:S(2)}) copy-start(f32[1536,192]{0,1:T(8,128)} %fusion) | copy-start | bytes 3538948
  103.9 6.2 %copy-start.2 = (f32[1536,192]{0,1:T(8,128)S(1)}, f32[1536,192]{0,1:T(8,128)}, u32[]{:S(2)}) copy-start(f32[1536,192]{0,1:T(8,128)} %fusion.18) | copy-start | bytes 3538948
  203.3 10.5 %all-to-all-start.3 = ((f32[8,192,32]{1,2,0:T(8,128)}), f32[8,192,32]{1,2,0:T(8,128)S(1)}, u32[]{:S(2)}, u32[]{:S(2)}) async-start(f32[8,192,32]{1,2,0:T(8,128)} %broadcast_in_dim.61), calls=%async_computation.3 | async-start | bytes 524288 | tf_op jit(solution)/shard_map/all_to_all | solution.py:26
  327.0 10.5 %all-to-all-start.12 = ((f32[8,192,32]{1,2,0:T(8,128)}), f32[8,192,32]{1,2,0:T(8,128)S(1)}, u32[]{:S(2)}, u32[]{:S(2)}) async-start(f32[8,192,32]{1,2,0:T(8,128)} %broadcast_in_dim.70), calls=%async_computation.12 | async-start | bytes 524288 | tf_op jit(solution)/shard_map/all_to_all | solution.py:26
Sparse Core Ops, SparseCore 0:
  9.7 71.0 all-gather.1
where the time goes:
time: 346 us; the launch traced here: 345 us
  blocking collectives  164 us (47%)
  waiting for transfers between devices  73.8 us (21%)
  other arithmetic  43.6 us (13%)
  matrix products  31.7 us (9%)
  between operations  14.5 us (4%)
  local copies, waits for them, and re-layouts  9.96 us (3%)
  starting transfers between devices  8.13 us (2%)
    all_to_all x10, blocking collectives, from_everyone(): return lax.all_to_all(copies, axis, split_axis=0, concat_axis=0, tiled=True)  109 us
    all_gather x1, waiting for transfers between devices, local(): gathered = lax.all_gather(coefs, 'row', axis=1, tiled=True)  61 us
    all_to_all x1, blocking collectives, sum_at_owner(): lax.all_to_all(tiles, axis, split_axis=0, concat_axis=0, tiled=True)  54.3 us
    dot_general x3, matrix products, inner(): lax.dot_general(left, right, (((1,), (1,)), ((), ())), precision=HIGH, pr...  29.2 us
    another operation x12, other arithmetic, local(): factor = jnp.linalg.cholesky(gram)  14.4 us
    another operation x8, other arithmetic, local(): lax.linalg.triangular_solve(factor, summed_rows, left_side=False, lower=T...  12.3 us
    all_to_all x2, waiting for transfers between devices, from_everyone(): return lax.all_to_all(copies, axis, split_axis=0, concat_axis=0, tiled=True)  12.1 us
    mul x2, other arithmetic, prepare(): paired = jnp.concatenate([values[0] * masks, values[1] * masks], axis=1)  10.3 us
  transfers between devices with their start and end apart: 3, of which 3 were waited for; matrix products, arithmetic and copies ran while one was open for 4% of the time, Pallas kernels for 0%

commit v1 on v0

--- a/solution.py
+++ b/solution.py
@@ -72,7 +72,9 @@
     own_tilts = lax.dynamic_slice_in_dim(tilts, row_index * row_count, row_count, 0)
     wave_index = col_index * slice_width + jnp.arange(slice_width, dtype=jnp.int32)
     own_mask, own_pair, own_energy = prepare(coefs, own_tilts, wave_index)
-    gathered = lax.all_gather(coefs, "row", axis=1, tiled=True)
+    gathered = jnp.concatenate(
+        lax.all_to_all(jnp.stack([coefs] * lax.axis_size("row")), "row", 0, 0), axis=1
+    )
     mask_j, pair_j, energy_j = prepare(gathered, tilts, wave_index)
     numer = inner(pair_j, own_pair)
     first = inner(mask_j, own_energy)

time: 346 us -> 418 us (1.21)
  waiting for transfers between devices: 73.8 us -> 144 us
  local copies, waits for them, and re-layouts: 9.96 us -> 27.7 us
  between operations: 14.5 us -> 1.09 us
  starting transfers between devices: 8.13 us -> 15 us
  matrix products: 31.7 us -> 25.9 us
    all_to_all x0 -> x1, waiting for transfers between devices: none -> 132 us  [local(): lax.all_to_all(jnp.stack([coefs] * lax.axis_size('row')), 'row', 0, 0)]
    all_gather x1 -> x0, waiting for transfers between devices: 61 us -> none  [local(): gathered = lax.all_gather(coefs, 'row', axis=1, tiled=True)]
    slice x0 -> x1, local copies, waits for them, and re-layouts: none -> 11.8 us  [prepare(): paired = jnp.concatenate([values[0] * masks, values[1] * masks], axis=1)]
    another operation x0 -> x1, local copies, waits for them, and re-layouts: none -> 7.51 us  [local(): jnp.stack([coefs] * lax.axis_size('row'))]
    all_to_all x0 -> x1, starting transfers between devices: none -> 6.93 us  [local(): lax.all_to_all(jnp.stack([coefs] * lax.axis_size('row')), 'row', 0, 0)]
    dot_general x3, matrix products: 29.2 us -> 23.4 us  [inner(): lax.dot_general(left, right, (((1,), (1,)), ((), ())), precision=HIGH, pr...]
  transfers between devices with their start and end apart: 3 -> 3, of which waited for: 3 -> 3; matrix products, arithmetic and copies ran while one was open for 4% -> 2% of each run, Pallas kernels for 0% -> 0%
where the time goes in v1:
time: 418 us; the launch traced here: 417 us
  blocking collectives  162 us (39%)
  waiting for transfers between devices  144 us (34%)
  other arithmetic  40.7 us (10%)
  local copies, waits for them, and re-layouts  27.7 us (7%)
  matrix products  25.9 us (6%)
  starting transfers between devices  15 us (4%)
    all_to_all x1, waiting for transfers between devices, local(): lax.all_to_all(jnp.stack([coefs] * lax.axis_size('row')), 'row', 0, 0)  132 us
    all_to_all x10, blocking collectives, from_everyone(): return lax.all_to_all(copies, axis, split_axis=0, concat_axis=0, tiled=True)  109 us
    all_to_all x1, blocking collectives, sum_at_owner(): lax.all_to_all(tiles, axis, split_axis=0, concat_axis=0, tiled=True)  53.3 us
    dot_general x3, matrix products, inner(): lax.dot_general(left, right, (((1,), (1,)), ((), ())), precision=HIGH, pr...  23.4 us
    another operation x12, other arithmetic, local(): factor = jnp.linalg.cholesky(gram)  14.4 us
    another operation x8, other arithmetic, local(): lax.linalg.triangular_solve(factor, summed_rows, left_side=False, lower=T...  12.3 us
    all_to_all x2, waiting for transfers between devices, from_everyone(): return lax.all_to_all(copies, axis, split_axis=0, concat_axis=0, tiled=True)  12.1 us
    slice x1, local copies, waits for them, and re-layouts, prepare(): paired = jnp.concatenate([values[0] * masks, values[1] * masks], axis=1)  11.8 us
  transfers between devices with their start and end apart: 3, of which 3 were waited for; matrix products, arithmetic and copies ran while one was open for 2% of the time, Pallas kernels for 0%

profile of v1, /device:TPU:1, one launch (start us, length us, event | category | flops | bytes accessed | tf_op | source)
XLA Modules:
  0.0 417.0 jit_solution(1593609482043462863)
XLA Ops:
  0.6 7.5 %stack.2 = f32[8,2,192,1024]{3,2,1,0:T(8,128)} broadcast(f32[2,192,1024]{2,1,0:T(8,128)} %param.6), dimensions={1,2,3} | broadcast | bytes 14155776 | tf_op jit(solution)/shard_map/stack | solution.py:76
  8.2 6.9 %all-to-all-start = ((f32[8,2,192,1024]{3,2,1,0:T(8,128)}), f32[8,2,192,1024]{3,2,1,0:T(8,128)}, u32[]{:S(2)}, u32[]{:S(2)}) async-start(f32[8,2,192,1024]{3,2,1,0:T(8,128)} %stack.2), calls=%async_computation | async-start | bytes 25165824 | tf_op jit(solution)/shard_map/all_to_all | solution.py:76
  15.6 6.0 %fusion.12 = f32[1536,192]{0,1:T(8,128)} fusion(f32[2,192,1024]{2,1,0:T(8,128)S(1)} %copy-done.1, s32[192]{0:T(256)S(1)} %bitcast.107, s32[1024]{0:T(1024)S(1)} %get-tuple-element.24, s32[1024]{0:T(1024)S(1)} %get-tuple-element.23, s32[192]{0:T(256)S(1)} %bitcast.104, s32[1024]{0:T(1024)S(1)} %broadcast_multiply_fusion, ...), kind=kOutput, calls=%fused_computation.25 | convolution fusion | flops 3633512448 | bytes 2797568 | tf_op jit(solution)/shard_map/dot_general | solution.py:52
  21.6 132.0 %all-to-all-done = f32[8,2,192,1024]{3,2,1,0:T(8,128)} async-done(((f32[8,2,192,1024]{3,2,1,0:T(8,128)}), f32[8,2,192,1024]{3,2,1,0:T(8,128)}, u32[]{:S(2)}, u32[]{:S(2)}) %all-to-all-start) | async-done | bytes 12582944 | tf_op jit(solution)/shard_map/all_to_all | solution.py:76
  153.6 11.8 %fusion.63 = (f32[1,8,192,1024]{3,2,0,1:T(8,128)}, f32[1,8,192,1024]{3,2,0,1:T(8,128)}) fusion(f32[2,8,192,1024]{3,2,0,1:T(8,128)} %bitcast), kind=kLoop, calls=%fused_computation.107 | loop fusion | bytes 25165824 | tf_op jit(solution)/shard_map/slice | solution.py:59
  165.4 7.0 %bitcast_select_fusion.1 = (f32[1536,1024]{1,0:T(8,128)S(1)}, f32[1536,1024]{1,0:T(8,128)S(1)}, f32[1536,1024]{1,0:T(8,128)S(1)}) fusion(f32[1,8,192,1024]{3,2,0,1:T(8,128)} %get-tuple-element.14, s32[1536]{0:T(1024)S(1)} %get-tuple-element.13, s32[1024]{0:T(1024)S(1)} %get-tuple-element.24, s32[1024]{0:T(1024)S(1)} %get-tuple-element.23, ...), kind=kLoop, calls=%fused_computation.9 | loop fusion | flops 17301504 | bytes 31482880 | tf_op jit(solution)/shard_map/mul | solution.py:59
  172.4 3.9 fusion.59
  176.4 13.5 %fusion = f32[1536,192]{0,1:T(8,128)S(1)} fusion(f32[1536,1024]{1,0:T(8,128)S(1)} %get-tuple-element.18, f32[1536,1024]{1,0:T(8,128)S(1)} %get-tuple-element.16, f32[192,1024]{1,0:T(8,128)S(1)} %get-tuple-element.20, f32[192,1024]{1,0:T(8,128)S(1)} %get-tuple-element.19), kind=kOutput, calls=%fused_computation | convolution fusion | flops 7251296256 | bytes 15335424 | tf_op jit(solution)/shard_map/dot_general | solution.py:52
  190.1 3.1 copy.54
  193.3 53.3 %all_to_all.70 = f32[16,96,576]{2,1,0:T(8,128)} all-to-all(f32[16,96,576]{2,1,0:T(8,128)} %bitcast.102), channel_id=1, replica_groups=mesh['row'=8,'col'=16] {'col'}, dimensions={0} | all-to-all | bytes 7077888 | tf_op jit(solution)/shard_map/all_to_all | solution.py:20
  249.3 12.3 %all_to_all.71 = f32[16,192,32]{1,2,0:T(8,128)S(1)} all-to-all(f32[16,192,32]{1,2,0:T(8,128)S(1)} %broadcast_in_dim.59), channel_id=1, replica_groups=mesh['row'=8,'col'=16] {'col'}, dimensions={0} | all-to-all | bytes 786432 | tf_op jit(solution)/shard_map/all_to_all | solution.py:26
  262.0 10.8 %all_to_all.72 = f32[8,1,1024]{2,1,0:T(1,128)S(1)} all-to-all(f32[8,1,1024]{2,1,0:T(1,128)S(1)} %reshape.109), channel_id=1, replica_groups=mesh['row'=8,'col'=16] {'row'}, dimensions={0} | all-to-all | bytes 65536 | tf_op jit(solution)/shard_map/all_to_all | solution.py:26
  274.2 2.9 cholesky.74
  278.5 2.4 custom-call.8
  281.9 4.0 all-to-all-start.4
  285.9 6.5 %all-to-all-done.4 = f32[8,192,32]{1,2,0:T(8,128)S(1)} async-done(((f32[8,192,32]{1,2,0:T(8,128)}), f32[8,192,32]{1,2,0:T(8,128)S(1)}, u32[]{:S(2)}, u32[]{:S(2)}) %all-to-all-start.4) | async-done | bytes 196640 | tf_op jit(solution)/shard_map/all_to_all | solution.py:26
  293.0 13.0 %all_to_all.73 = f32[16,192,32]{1,2,0:T(8,128)S(1)} all-to-all(f32[16,192,32]{1,2,0:T(8,128)S(1)} %broadcast_in_dim.62), channel_id=1, replica_groups=mesh['row'=8,'col'=16] {'col'}, dimensions={0} | all-to-all | bytes 786432 | tf_op jit(solution)/shard_map/all_to_all | solution.py:26
  306.4 9.2 %all_to_all.74 = f32[8,1,1024]{2,1,0:T(1,128)S(1)} all-to-all(f32[8,1,1024]{2,1,0:T(1,128)S(1)} %reshape.111), channel_id=1, replica_groups=mesh['row'=8,'col'=16] {'row'}, dimensions={0} | all-to-all | bytes 65536 | tf_op jit(solution)/shard_map/all_to_all | solution.py:26
  316.5 2.9 cholesky.85
  320.8 2.4 custom-call.9
  323.5 9.6 %all_to_all.75 = f32[8,192,32]{1,2,0:T(8,128)S(1)} all-to-all(f32[8,192,32]{1,2,0:T(8,128)S(1)} %broadcast_in_dim.64), channel_id=1, replica_groups=mesh['row'=8,'col'=16] {'row'}, dimensions={0} | all-to-all | bytes 393216 | tf_op jit(solution)/shard_map/all_to_all | solution.py:26
  333.7 13.0 %all_to_all.76 = f32[16,192,32]{1,2,0:T(8,128)S(1)} all-to-all(f32[16,192,32]{1,2,0:T(8,128)S(1)} %broadcast_in_dim.65), channel_id=1, replica_groups=mesh['row'=8,'col'=16] {'col'}, dimensions={0} | all-to-all | bytes 786432 | tf_op jit(solution)/shard_map/all_to_all | solution.py:26
  347.1 9.2 %all_to_all.77 = f32[8,1,1024]{2,1,0:T(1,128)S(1)} all-to-all(f32[8,1,1024]{2,1,0:T(1,128)S(1)} %reshape.113), channel_id=1, replica_groups=mesh['row'=8,'col'=16] {'row'}, dimensions={0} | all-to-all | bytes 65536 | tf_op jit(solution)/shard_map/all_to_all | solution.py:26
  357.2 2.9 cholesky.96
  361.5 2.4 custom-call.10
  364.2 9.6 %all_to_all.78 = f32[8,192,32]{1,2,0:T(8,128)S(1)} all-to-all(f32[8,192,32]{1,2,0:T(8,128)S(1)} %broadcast_in_dim.67), channel_id=1, replica_groups=mesh['row'=8,'col'=16] {'row'}, dimensions={0} | all-to-all | bytes 393216 | tf_op jit(solution)/shard_map/all_to_all | solution.py:26
  374.4 13.0 %all_to_all.79 = f32[16,192,32]{1,2,0:T(8,128)S(1)} all-to-all(f32[16,192,32]{1,2,0:T(8,128)S(1)} %broadcast_in_dim.68), channel_id=1, replica_groups=mesh['row'=8,'col'=16] {'col'}, dimensions={0} | all-to-all | bytes 786432 | tf_op jit(solution)/shard_map/all_to_all | solution.py:26
  387.7 9.2 %all_to_all.80 = f32[8,1,1024]{2,1,0:T(1,128)S(1)} all-to-all(f32[8,1,1024]{2,1,0:T(1,128)S(1)} %reshape.115), channel_id=1, replica_groups=mesh['row'=8,'col'=16] {'row'}, dimensions={0} | all-to-all | bytes 65536 | tf_op jit(solution)/shard_map/all_to_all | solution.py:26
  397.9 2.9 cholesky.107
  402.1 2.4 custom-call.11
  405.5 4.0 all-to-all-start.13
  410.4 5.6 %all-to-all-done.13 = f32[8,192,32]{1,2,0:T(8,128)S(1)} async-done(((f32[8,192,32]{1,2,0:T(8,128)}), f32[8,192,32]{1,2,0:T(8,128)S(1)}, u32[]{:S(2)}, u32[]{:S(2)}) %all-to-all-start.13) | async-done | bytes 196640 | tf_op jit(solution)/shard_map/all_to_all | solution.py:26
  (93 shorter events, 20.1 us)
Async XLA Ops:
  0.6 248.4 %copy-start = (f32[96,32]{0,1:T(8,128)S(1)}, f32[96,32]{0,1:T(8,128)}, u32[]{:S(2)}) copy-start(f32[96,32]{0,1:T(8,128)} %param.8) | copy-start | bytes 36868
  8.2 7.0 %copy-start.3 = (s32[1536,2]{0,1:T(2,128)S(1)}, s32[1536,2]{0,1:T(2,128)}, u32[]{:S(2)}) copy-start(s32[1536,2]{0,1:T(2,128)} %param.7) | copy-start | bytes 36868
  8.2 7.1 %copy-start.1 = (f32[2,192,1024]{2,1,0:T(8,128)S(1)}, f32[2,192,1024]{2,1,0:T(8,128)}, u32[]{:S(2)}) copy-start(f32[2,192,1024]{2,1,0:T(8,128)} %param.6) | copy-start | bytes 4718596
  8.2 145.5 %all-to-all-start = ((f32[8,2,192,1024]{3,2,1,0:T(8,128)}), f32[8,2,192,1024]{3,2,1,0:T(8,128)}, u32[]{:S(2)}, u32[]{:S(2)}) async-start(f32[8,2,192,1024]{3,2,1,0:T(8,128)} %stack.2), calls=%async_computation | async-start | bytes 25165824 | tf_op jit(solution)/shard_map/all_to_all | solution.py:76
  176.3 13.5 %copy-start.2 = (f32[1536,192]{0,1:T(8,128)S(1)}, f32[1536,192]{0,1:T(8,128)}, u32[]{:S(2)}) copy-start(f32[1536,192]{0,1:T(8,128)} %fusion.12) | copy-start | bytes 3538948
  281.9 10.5 %all-to-all-start.4 = ((f32[8,192,32]{1,2,0:T(8,128)}), f32[8,192,32]{1,2,0:T(8,128)S(1)}, u32[]{:S(2)}, u32[]{:S(2)}) async-start(f32[8,192,32]{1,2,0:T(8,128)} %broadcast_in_dim.61), calls=%async_computation.4 | async-start | bytes 524288 | tf_op jit(solution)/shard_map/all_to_all | solution.py:26
  405.5 10.5 %all-to-all-start.13 = ((f32[8,192,32]{1,2,0:T(8,128)}), f32[8,192,32]{1,2,0:T(8,128)S(1)}, u32[]{:S(2)}, u32[]{:S(2)}) async-start(f32[8,192,32]{1,2,0:T(8,128)} %broadcast_in_dim.70), calls=%async_computation.13 | async-start | bytes 524288 | tf_op jit(solution)/shard_map/all_to_all | solution.py:26
